TPU v7x, 256 devices: a whole 4x4x8 slice. The times are simulated.
256 devices in a mesh: mrow: 8 (over y, z_lo), pcol: 32 (over x, z_hi, core).
Axes of the slice: x: 4, y: 4, z: 8 (z_hi: 4, z_lo: 2; z = z_hi * 2 + z_lo), core: 2. Of those that a mesh axis runs over, the one named last changes fastest.
Arguments:
- snapshots: bfloat16 [7424, 8192], P('mrow', 'pcol'), may hold values from -16 to 16
- area_weight: float32 [8192], P('pcol'), may hold values from 0.2 to 1
Outputs:
- gram_tiles: float32 [8, 32, 215296], P('mrow', 'pcol')
All inputs are finite; a program needn't handle non-finite values.
Results may differ from a plain program's by a relative error of at most 0.0003.
Values may be sent and summed in bfloat16 or wider, within the bound.
A program may use at most 64 MiB of HBM per device.

v0:
```python
import jax
import jax.numpy as jnp
from jax import lax
from jax.sharding import Mesh
from jax.sharding import PartitionSpec as P

MEMBERS = 7424
MROW = ("mrow_0", "mrow_1")


def sent_to_all(value, axis):
    copies = jnp.broadcast_to(value, (lax.axis_size(axis), *value.shape))
    return lax.all_to_all(copies, axis, split_axis=0, concat_axis=0, tiled=True)


def of_everyone(value, axis):
    everything = sent_to_all(value, axis)
    return jnp.sum(everything, axis=0)


def gather_axes(value, axes, dim):
    for axis in reversed(axes):
        value = lax.all_gather(value, axis, axis=dim, tiled=True)
    return value


def local(snapshots, area_weight):
    member_rows = snapshots.shape[0]
    ratio = lax.axis_size("pcol") // lax.axis_size(MROW)
    tile = member_rows // ratio
    local_sum = jnp.sum(snapshots.astype(jnp.float32), axis=0)
    ens_mean = of_everyone(local_sum, MROW) / MEMBERS
    anomaly = (
        (snapshots.astype(jnp.float32) - ens_mean[None, :]) * jnp.sqrt(area_weight)[None, :]
    ).astype(jnp.bfloat16)
    contract = (((1,), (1,)), ((), ()))
    every_member = gather_axes(anomaly, MROW, 0)
    col_block = lax.all_to_all(every_member, "pcol", split_axis=0, concat_axis=1, tiled=True)
    gram = lax.dot_general(
        lax.all_gather(anomaly, "pcol", axis=1, tiled=True),
        col_block,
        contract,
        preferred_element_type=jnp.float32,
    )
    gram = gram / (MEMBERS - 1)
    return gram.reshape(1, 1, member_rows * tile)


def solution(mesh):
    torus = Mesh(mesh.devices.reshape(4, 2, mesh.shape["pcol"]), ("mrow_0", "mrow_1", "pcol"))
    return jax.shard_map(
        local,
        mesh=torus,
        in_specs=(P(MROW, "pcol"), P("pcol")),
        out_specs=P(MROW, "pcol", None),
        check_vma=False,
    )
```

profile of v0, /device:TPU:1, one launch (start us, length us, event | category | flops | bytes accessed | tf_op | source)
XLA Modules:
  0.0 288.2 jit_solution(7553588986702876311)
XLA Ops:
  6.5 1.2 convert_reduce_fusion
  7.7 0.6 broadcast_in_dim.2
  8.3 6.4 %all-to-all-start = ((f32[8,1,256]{2,1,0:T(1,128)}), f32[8,1,256]{2,1,0:T(1,128)S(1)}, u32[]{:S(2)}, u32[]{:S(2)}) async-start(f32[8,1,256]{2,1,0:T(1,128)} %broadcast_in_dim.2), calls=%async_computation | async-start | bytes 16384 | tf_op jit(solution)/shard_map/all_to_all | solution.py:13
  14.7 0.0 all-gather.5.cloned.1.call-start
  14.7 0.7 sqrt.3
  15.4 4.3 %all-to-all-done = f32[8,1,256]{2,1,0:T(1,128)S(1)} async-done(((f32[8,1,256]{2,1,0:T(1,128)}), f32[8,1,256]{2,1,0:T(1,128)S(1)}, u32[]{:S(2)}, u32[]{:S(2)}) %all-to-all-start) | async-done | bytes 8224 | tf_op jit(solution)/shard_map/all_to_all | solution.py:13
  19.7 1.1 fusion.1
  20.9 0.0 copy-start
  20.9 11.1 %all_gather.10 = bf16[1856,256]{1,0:T(8,128)(2,1)} all-gather(bf16[928,256]{1,0:T(8,128)(2,1)S(1)} %fusion.1), channel_id=1, replica_groups=mesh['mrow_0'=4,'mrow_1'=2,'pcol'=32] {'mrow_1'}, dimensions={0}, use_global_device_ids=true | all-gather | bytes 1425408 | tf_op jit(solution)/shard_map/all_gather | solution.py:23
  32.0 0.0 all-gather.5.cloned.1.call-update
  32.0 0.0 all-gather.3.cloned.1.call-start
  32.1 0.0 copy-done
  32.1 0.7 all-gather.3.cloned.1.call-update
  32.8 49.1 %all-gather.5.cloned.1.call-done = bf16[7424,256]{1,0:T(8,128)(2,1)} async-done(((bf16[1856,256]{1,0:T(8,128)(2,1)}), bf16[7424,256]{1,0:T(8,128)(2,1)}) %all-gather.5.cloned.1.call-update) | async-done | bytes 3801104 | tf_op jit(solution)/shard_map/all_gather | solution.py:23
  81.9 113.8 %all_to_all.25 = bf16[32,232,256]{2,1,0:T(8,128)(2,1)S(1)} all-to-all(bf16[32,232,256]{2,1,0:T(8,128)(2,1)} %bitcast.7), channel_id=1, replica_groups=mesh['mrow_0'=4,'mrow_1'=2,'pcol'=32] {'pcol'}, dimensions={0} | all-to-all | bytes 7602176 | tf_op jit(solution)/shard_map/all_to_all | solution.py:38
  195.7 2.3 copy.9
  198.0 72.2 %all-gather.3.cloned.1.call-done = bf16[928,8192]{1,0:T(8,128)(2,1)} async-done(((bf16[928,256]{1,0:T(8,128)(2,1)}), bf16[928,8192]{1,0:T(8,128)(2,1)}) %all-gather.3.cloned.1.call-update) | async-done | bytes 15204368 | tf_op jit(solution)/shard_map/all_gather | solution.py:40
  270.3 8.6 %convolution_multiply_fusion = f32[928,232]{1,0:T(8,128)S(1)} fusion(bf16[928,8192]{1,0:T(8,128)(2,1)} %all-gather.3.cloned.1.call-done, bf16[232,8192]{1,0:T(8,128)(2,1)} %bitcast.8), kind=kOutput, calls=%fused_computation | convolution fusion | flops 3527624960 | bytes 19866624 | tf_op jit(solution)/shard_map/dot_general | solution.py:39
  278.8 2.6 reshape.14
  (2 shorter events, 0.0 us)
Async XLA Ops:
  8.3 11.4 %all-to-all-start = ((f32[8,1,256]{2,1,0:T(1,128)}), f32[8,1,256]{2,1,0:T(1,128)S(1)}, u32[]{:S(2)}, u32[]{:S(2)}) async-start(f32[8,1,256]{2,1,0:T(1,128)} %broadcast_in_dim.2), calls=%async_computation | async-start | bytes 16384 | tf_op jit(solution)/shard_map/all_to_all | solution.py:13
  14.7 67.2 %all-gather.5.cloned.1.call-start = ((), (), s32[]{:S(2)}) async-start(), calls=%async_computation.3 | async-start | bytes 4751360 | tf_op jit(solution)/shard_map/all_gather | solution.py:23
  20.9 11.2 %copy-start = (bf16[928,256]{1,0:T(8,128)(2,1)}, bf16[928,256]{1,0:T(8,128)(2,1)S(1)}, u32[]{:S(2)}) copy-start(bf16[928,256]{1,0:T(8,128)(2,1)S(1)} %fusion.1) | copy-start | bytes 1425412
  32.0 238.2 %all-gather.3.cloned.1.call-start = ((), (), s32[]{:S(2)}) async-start(), calls=%async_computation.2 | async-start | bytes 15679488 | tf_op jit(solution)/shard_map/all_gather | solution.py:40
Sparse Core Ops, SparseCore 0:
  32.1 49.6 all-gather.4
  84.3 185.8 all-gather.2
where the time goes:
time: 289 us; the launch traced here: 288 us
  waiting for transfers between devices  126 us (44%)
  blocking collectives  125 us (43%)
  between operations  13.4 us (5%)
  matrix products  8.57 us (3%)
  starting transfers between devices  6.44 us (2%)
  local copies, waits for them, and re-layouts  6.17 us (2%)
    all_to_all x1, blocking collectives, local(): lax.all_to_all(every_member, 'pcol', split_axis=0, concat_axis=1, tiled=T...  114 us
    all_gather x1, waiting for transfers between devices, local(): lax.all_gather(anomaly, 'pcol', axis=1, tiled=True)  72.2 us
    all_gather x1, waiting for transfers between devices, gather_axes(): value = lax.all_gather(value, axis, axis=dim, tiled=True)  49.1 us
    all_gather x1, blocking collectives, gather_axes(): value = lax.all_gather(value, axis, axis=dim, tiled=True)  11.1 us
    dot_general x1, matrix products, local(): lax.dot_general(lax.all_gather(anomaly, 'pcol', axis=1, tiled=True), col_...  8.57 us
    all_to_all x1, starting transfers between devices, sent_to_all(): return lax.all_to_all(copies, axis, split_axis=0, concat_axis=0, tiled=True)  6.36 us
  transfers between devices with their start and end apart: 3, of which 3 were waited for; matrix products, arithmetic and copies ran while one was open for 1% of the time, Pallas kernels for 0%

commit v1 on v0

--- a/solution.py
+++ b/solution.py
@@ -6,6 +6,13 @@
 
 MEMBERS = 7424
 MROW = ("mrow_0", "mrow_1")
+
+
+def all_by_exchange(array, name, along):
+    peers = lax.axis_size(name)
+    pieces = jnp.stack([array for _ in range(peers)])
+    pieces = lax.all_to_all(pieces, name, split_axis=0, concat_axis=0)
+    return jnp.concatenate(pieces, axis=along)
 
 
 def sent_to_all(value, axis):
@@ -37,10 +44,7 @@
     every_member = gather_axes(anomaly, MROW, 0)
     col_block = lax.all_to_all(every_member, "pcol", split_axis=0, concat_axis=1, tiled=True)
     gram = lax.dot_general(
-        lax.all_gather(anomaly, "pcol", axis=1, tiled=True),
-        col_block,
-        contract,
-        preferred_element_type=jnp.float32,
+        all_by_exchange(anomaly, "pcol", 1), col_block, contract, preferred_element_type=jnp.float32
     )
     gram = gram / (MEMBERS - 1)
     return gram.reshape(1, 1, member_rows * tile)

time: 289 us -> 539 us (1.87)
  blocking collectives: 125 us -> 448 us
  waiting for transfers between devices: 126 us -> 54.2 us
    all_to_all x0 -> x1, blocking collectives: none -> 338 us  [all_by_exchange(): pieces = lax.all_to_all(pieces, name, split_axis=0, concat_axis=0)]
    all_gather x1 -> x0, waiting for transfers between devices: 72.2 us -> none  [local(): lax.all_gather(anomaly, 'pcol', axis=1, tiled=True)]
    all_to_all x1, blocking collectives: 114 us -> 98.8 us  [local(): lax.all_to_all(every_member, 'pcol', split_axis=0, concat_axis=1, tiled=T...]
    another operation x0 -> x1, local copies, waits for them, and re-layouts: none -> 7.05 us  [all_by_exchange(): pieces = jnp.stack([array for _ in range(peers)])]
  transfers between devices with their start and end apart: 3 -> 2, of which waited for: 3 -> 2; matrix products, arithmetic and copies ran while one was open for 1% -> 0% of each run, Pallas kernels for 0% -> 0%
where the time goes in v1:
time: 539 us
  blocking collectives  448 us (83%)
  waiting for transfers between devices  54.2 us (10%)
  between operations  13.4 us (2%)
  local copies, waits for them, and re-layouts  10.9 us (2%)
  starting transfers between devices  6.4 us (1%)
    all_to_all x1, blocking collectives, all_by_exchange(): pieces = lax.all_to_all(pieces, name, split_axis=0, concat_axis=0)  338 us
    all_to_all x1, blocking collectives, local(): lax.all_to_all(every_member, 'pcol', split_axis=0, concat_axis=1, tiled=T...  98.8 us
    all_gather x1, waiting for transfers between devices, gather_axes(): value = lax.all_gather(value, axis, axis=dim, tiled=True)  49.9 us
    all_gather x1, blocking collectives, gather_axes(): value = lax.all_gather(value, axis, axis=dim, tiled=True)  11.1 us
  transfers between devices with their start and end apart: 2, of which 2 were waited for; matrix products, arithmetic and copies ran while one was open for 0% of the time, Pallas kernels for 0%

profile of v1, /device:TPU:1, one launch (start us, length us, event | category | flops | bytes accessed | tf_op | source)
XLA Modules:
  0.0 539.1 jit_solution(11721172851158314472)
XLA Ops:
  6.5 1.2 convert_reduce_fusion
  7.7 0.6 broadcast_in_dim.2
  8.3 6.4 %all-to-all-start = ((f32[8,1,256]{2,1,0:T(1,128)}), f32[8,1,256]{2,1,0:T(1,128)S(1)}, u32[]{:S(2)}, u32[]{:S(2)}) async-start(f32[8,1,256]{2,1,0:T(1,128)} %broadcast_in_dim.2), calls=%async_computation | async-start | bytes 16384 | tf_op jit(solution)/shard_map/all_to_all | solution.py:20
  14.7 0.0 all-gather.2.cloned.1.call-start
  14.7 0.7 sqrt.3
  15.4 4.3 all-to-all-done
  19.7 1.1 fusion.14
  20.9 11.1 %all_gather.6 = bf16[1856,256]{1,0:T(8,128)(2,1)} all-gather(bf16[928,256]{1,0:T(8,128)(2,1)S(1)} %fusion.14), channel_id=1, replica_groups=mesh['mrow_0'=4,'mrow_1'=2,'pcol'=32] {'mrow_1'}, dimensions={0}, use_global_device_ids=true | all-gather | bytes 1425408 | tf_op jit(solution)/shard_map/all_gather | solution.py:30
  32.0 0.0 all-gather.2.cloned.1.call-update
  32.0 49.9 %all-gather.2.cloned.1.call-done = bf16[7424,256]{1,0:T(8,128)(2,1)} async-done(((bf16[1856,256]{1,0:T(8,128)(2,1)}), bf16[7424,256]{1,0:T(8,128)(2,1)}) %all-gather.2.cloned.1.call-update) | async-done | bytes 3801104 | tf_op jit(solution)/shard_map/all_gather | solution.py:30
  81.9 98.8 %all_to_all.27 = bf16[32,232,256]{2,1,0:T(8,128)(2,1)} all-to-all(bf16[32,232,256]{2,1,0:T(8,128)(2,1)} %bitcast.19), channel_id=1, replica_groups=mesh['mrow_0'=4,'mrow_1'=2,'pcol'=32] {'pcol'}, dimensions={0} | all-to-all | bytes 7602176 | tf_op jit(solution)/shard_map/all_to_all | solution.py:45
  180.7 7.1 %stack.2 = bf16[32,928,256]{2,1,0:T(8,128)(2,1)} broadcast(bf16[928,256]{1,0:T(8,128)(2,1)S(1)} %fusion.14), dimensions={1,2} | broadcast | bytes 15679488 | tf_op jit(solution)/shard_map/stack | solution.py:13
  187.7 0.0 copy-start
  187.7 337.9 %all_to_all.28 = bf16[32,928,256]{2,1,0:T(8,128)(2,1)S(1)} all-to-all(bf16[32,928,256]{2,1,0:T(8,128)(2,1)} %stack.2), channel_id=1, replica_groups=mesh['mrow_0'=4,'mrow_1'=2,'pcol'=32] {'pcol'}, dimensions={0} | all-to-all | bytes 30408704 | tf_op jit(solution)/shard_map/all_to_all | solution.py:14
  525.6 0.0 copy-done
  525.6 4.1 fusion.8
  529.7 2.6 reshape.21
  (2 shorter events, 0.0 us)
Async XLA Ops:
  8.3 11.4 %all-to-all-start = ((f32[8,1,256]{2,1,0:T(1,128)}), f32[8,1,256]{2,1,0:T(1,128)S(1)}, u32[]{:S(2)}, u32[]{:S(2)}) async-start(f32[8,1,256]{2,1,0:T(1,128)} %broadcast_in_dim.2), calls=%async_computation | async-start | bytes 16384 | tf_op jit(solution)/shard_map/all_to_all | solution.py:20
  14.7 67.2 %all-gather.2.cloned.1.call-start = ((), (), s32[]{:S(2)}) async-start(), calls=%async_computation.3 | async-start | bytes 4751360 | tf_op jit(solution)/shard_map/all_gather | solution.py:30
  187.7 337.9 %copy-start = (bf16[32,232,256]{2,1,0:T(8,128)(2,1)S(1)}, bf16[32,232,256]{2,1,0:T(8,128)(2,1)}, u32[]{:S(2)}) copy-start(bf16[32,232,256]{2,1,0:T(8,128)(2,1)} %all_to_all.27) | copy-start | bytes 11403268
Sparse Core Ops, SparseCore 0:
  32.1 49.6 all-gather.1
